TPU v7x, 32 devices: a whole 2x2x4 slice. The times are simulated.
32 devices in a mesh: head: 2 (over y), seq: 16 (over z, x, core).
Axes of the slice: x: 2, y: 2, z: 4, core: 2. Of those that a mesh axis runs over, the one named last changes fastest.
Arguments:
- queries: bfloat16 [2048, 4096], P(('seq', 'head')), may hold values from -20 to 20
- keys: bfloat16 [2048, 1024], P(('seq', 'head')), may hold values from -5 to 5
- values: bfloat16 [2048, 1024], P(('seq', 'head')), may hold values from -6 to 6
Outputs:
- attended: bfloat16 [2048, 4096], P(('seq', 'head'))
All inputs are finite; a program needn't handle non-finite values.
Results may differ from a plain program's by a relative error of at most 0.0041.
Values may be sent and summed in bfloat16 or wider, within the bound.
A program may use at most 64 MiB of HBM per device.

v0:
```python
import functools
import math

import jax
import jax.numpy as jnp
from jax import lax
from jax.experimental import pallas as pl
from jax.experimental.pallas import tpu as pltpu
from jax.sharding import PartitionSpec as P

HEAD_DIM = 128
TILE = 256
MESH = pl.DeviceIdType.MESH
NEG = -1e30


def kernel(
    cfg, q_in, k_in, v_in, out_ref, q_stage, kv_stage, q_all, kv_all, largest, summed, result,
    load_sem, own_sem, go_sem, kv_send, kv_recv, q_send, q_recv, rise_send, up_send, up_recv, out_send, out_recv,
):
    heads, planes, inner, group, rows, chunk = cfg
    members = heads * inner
    plane_rows = members * rows
    chunks = plane_rows // chunk
    width = group * HEAD_DIM
    seq = lax.axis_index("seq")
    head = lax.axis_index("head")
    plane = seq // inner
    me = (seq % inner) * heads + head
    has_up = plane < planes - 1
    has_down = plane > 0

    def member(g):
        return {"head": g % heads, "seq": plane * inner + g // heads}

    def other_plane(step):
        return {"head": head, "seq": seq + step * inner}

    turns = inner % 2 == 0
    core = seq % 2 if turns else 0
    first_turn = plane >= 0 if not turns else core == 0
    second_turn = plane < 0 if not turns else core == 1

    def flip(mask, start=me):
        g, bit = start, 1
        while bit < members:
            if mask & bit:
                g = g + bit * (1 - 2 * ((start // bit) % 2))
            bit *= 2
        return g

    def cols(g, size):
        return pl.ds(pl.multiple_of(g * size, HEAD_DIM), size)

    def block(g):
        return pl.ds(pl.multiple_of(g * rows, rows), rows)

    def position(g):
        return pl.ds(pl.multiple_of((plane * members + g) * rows, rows), rows)

    def piece(index):
        return pl.ds(pl.multiple_of(index * chunk, chunk), chunk)

    loads = [
        pltpu.make_async_copy(k_in, kv_stage.at[0], load_sem.at[0]),
        pltpu.make_async_copy(v_in, kv_stage.at[1], load_sem.at[1]),
        pltpu.make_async_copy(q_in, q_stage, load_sem.at[2]),
    ]
    own = [
        pltpu.make_async_copy(k_in.at[:, cols(me, HEAD_DIM)], kv_all.at[0, position(me)], own_sem.at[0]),
        pltpu.make_async_copy(v_in.at[:, cols(me, HEAD_DIM)], kv_all.at[1, position(me)], own_sem.at[1]),
        pltpu.make_async_copy(q_in.at[:, cols(me, width)], q_all.at[block(me)], own_sem.at[2]),
    ]
    for copy in loads + own:
        copy.start()

    barrier = pltpu.get_barrier_semaphore()
    for d in range(1, members):
        pl.semaphore_signal(
            barrier, inc=1, device_id=member((me + d) % members), device_id_type=MESH
        )

    @pl.when(has_up)
    def _():
        pl.semaphore_signal(barrier, inc=1, device_id=other_plane(1), device_id_type=MESH)

    @pl.when(has_down)
    def _():
        pl.semaphore_signal(barrier, inc=1, device_id=other_plane(-1), device_id_type=MESH)

    beside = jnp.minimum(plane, 1) + jnp.minimum(planes - 1 - plane, 1)
    pl.semaphore_wait(barrier, members - 1 + beside)

    def kv_copy(src, dst, to):
        return pltpu.make_async_remote_copy(
            src_ref=kv_stage.at[:, :, cols(dst, HEAD_DIM)],
            dst_ref=kv_all.at[:, position(src)],
            send_sem=kv_send.at[dst],
            recv_sem=kv_recv.at[src],
            device_id=member(to),
            device_id_type=MESH,
        )

    def q_copy(src, dst, to):
        return pltpu.make_async_remote_copy(
            src_ref=q_stage.at[:, cols(dst, width)],
            dst_ref=q_all.at[block(src)],
            send_sem=q_send.at[dst],
            recv_sem=q_recv.at[src],
            device_id=member(to),
            device_id_type=MESH,
        )

    def up_copy(index):
        return pltpu.make_async_remote_copy(
            src_ref=kv_all.at[:, piece(index)],
            dst_ref=kv_all.at[:, piece(index)],
            send_sem=up_send.at[index],
            recv_sem=up_recv.at[index],
            device_id=other_plane(1),
            device_id_type=MESH,
        )

    def rise_copy(src):
        return pltpu.make_async_remote_copy(
            src_ref=kv_all.at[:, position(src)],
            dst_ref=kv_all.at[:, position(src)],
            send_sem=rise_send.at[src],
            recv_sem=up_recv.at[plane * chunks + src // (members // chunks)],
            device_id=other_plane(1),
            device_id_type=MESH,
        )

    def out_copy(src, dst, to):
        return pltpu.make_async_remote_copy(
            src_ref=result.at[block(dst)],
            dst_ref=out_ref.at[:, cols(src, width)],
            send_sem=out_send.at[dst],
            recv_sem=out_recv.at[src],
            device_id=member(to),
            device_id_type=MESH,
        )

    far_first = sorted(range(members), key=lambda m: (m < members // 2, m % 2, m))
    near_first = sorted(range(members), key=lambda m: (m * chunks // members, m % 2, m))
    if turns:
        sends = sorted(far_first, key=lambda m: (m // heads) % 2)
    else:
        sends = far_first
    peers = [flip(mask, me - core * heads) for mask in sends]

    def start_all(copy_of):
        for to in peers:

            @pl.when(to != me)
            def _(to=to):
                copy_of(me, to, to).start()

    loads[0].wait()
    loads[1].wait()
    start_all(kv_copy)
    loads[2].wait()
    start_all(q_copy)

    for mask in near_first:
        src = flip(mask)
        if mask:
            kv_copy(src, me, src).wait_recv()
        else:
            own[0].wait()
            own[1].wait()

        @pl.when(has_up & first_turn)
        def _(src=src):
            rise_copy(src).start()

    def pass_turn(condition):
        if turns:

            @pl.when(has_up & first_turn & condition)
            def _():
                sibling = {"head": head, "seq": seq + 1}
                pl.semaphore_signal(go_sem, inc=1, device_id=sibling, device_id_type=MESH)

    pass_turn(plane <= 1)

    def receive(index):
        up_copy(index).wait_recv()

        @pl.when(has_up)
        def _():
            up_copy(index).start()

    per_chunk = members // chunks

    def nearest(c):
        return (me // per_chunk + c) % chunks

    if turns:

        @pl.when(has_up & second_turn)
        def _():
            pl.semaphore_wait(go_sem, 1)
            for mask in near_first:
                rise_copy(flip(mask)).start()

    ahead = jnp.minimum(plane, 1)
    if turns:
        ahead = jnp.where(first_turn, plane, ahead)
    ahead = jnp.where(has_up, ahead, 0)

    def forward(step, carry):
        for c in range(chunks):
            receive((plane - step) * chunks + nearest(c))
            if c == 0:
                pass_turn(step == plane - 1)
        return carry

    lax.fori_loop(1, ahead + 1, forward, 0)

    own[2].wait()
    for mask in range(1, members):
        src = flip(mask)
        q_copy(src, me, src).wait_recv()

    scale = math.log2(math.e) / math.sqrt(HEAD_DIM)
    ones = jnp.ones((chunk, HEAD_DIM), jnp.bfloat16)

    def attend(index, tiles, first, masked):
        keys = kv_all[0, piece(index), :]
        values = jnp.concatenate([kv_all[1, piece(index), :], ones], axis=1)
        for r in tiles:
            for j in range(group):
                q = q_all[r * chunk:(r + 1) * chunk, j * HEAD_DIM:(j + 1) * HEAD_DIM]
                at = slice(j * plane_rows + r * chunk, j * plane_rows + (r + 1) * chunk)
                score = lax.dot_general(
                    q, keys, (((1,), (1,)), ((), ())), preferred_element_type=jnp.float32
                )
                if r == masked:
                    row = lax.broadcasted_iota(jnp.int32, score.shape, 0)
                    col = lax.broadcasted_iota(jnp.int32, score.shape, 1)
                    score = jnp.where(col <= row, score, NEG)
                top = jnp.broadcast_to(jnp.max(score, axis=1, keepdims=True), (chunk, HEAD_DIM))
                if not first:
                    before = largest[at, :]
                    top = jnp.maximum(before, top)
                spread = jnp.concatenate([top] * (chunk // HEAD_DIM), axis=1)
                weight = jnp.exp2((score - spread) * scale).astype(jnp.bfloat16)
                product = jnp.dot(weight, values, preferred_element_type=jnp.float32)
                if first:
                    summed[at, :] = product
                else:
                    shrink = jnp.exp2((before - top) * scale)
                    summed[at, :] = summed[at, :] * jnp.concatenate([shrink, shrink], axis=1) + product
                largest[at, :] = top

    for c in range(chunks):
        attend(plane * chunks + c, range(c, chunks), c == 0, c)

    def earlier(step, carry):
        for c in range(chunks):
            index = (plane - step) * chunks + nearest(c)

            @pl.when(step > ahead)
            def _():
                receive(index)

            attend(index, range(chunks), False, -1)
        return carry

    lax.fori_loop(1, plane + 1, earlier, 0)

    def finish(g):
        for j in range(group):
            at = pl.ds(pl.multiple_of(j * plane_rows + g * rows, rows), rows)
            result[block(g), j * HEAD_DIM:(j + 1) * HEAD_DIM] = (
                summed[at, :HEAD_DIM] / summed[at, HEAD_DIM:]
            ).astype(jnp.bfloat16)

    for mask in far_first:
        to = flip(mask)
        finish(to)
        if mask:
            out_copy(me, to, to).start()
    keep = pltpu.make_async_copy(result.at[block(me)], out_ref.at[:, cols(me, width)], own_sem.at[3])
    keep.start()

    for d in range(1, members):
        to = (me + d) % members
        kv_copy(me, to, to).wait_send()
        q_copy(me, to, to).wait_send()

    @pl.when(has_up)
    def _():
        def sent(index, carry):
            up_copy(index).wait_send()
            return carry

        lax.fori_loop(0, plane * chunks, sent, 0)
        for mask in range(members):
            rise_copy(flip(mask)).wait_send()

    for d in range(1, members):
        src = (me + d) % members
        out_copy(src, me, src).wait_recv()
        out_copy(me, src, src).wait_send()
    keep.wait()


def solution(mesh):
    heads, seqs = mesh.shape["head"], mesh.shape["seq"]

    def on_device(queries, keys, values):
        rows = queries.shape[0]
        members = keys.shape[1] // HEAD_DIM
        inner = members // heads
        planes = seqs // inner
        group = queries.shape[1] // keys.shape[1]
        plane_rows = members * rows
        chunk = math.gcd(plane_rows, TILE)
        total = planes * plane_rows
        pieces = total // chunk
        dma = pltpu.SemaphoreType.DMA
        cfg = (heads, planes, inner, group, rows, chunk)
        return pl.pallas_call(
            functools.partial(kernel, cfg),
            out_shape=jax.ShapeDtypeStruct(queries.shape, jnp.bfloat16),
            in_specs=[pl.BlockSpec(memory_space=pl.ANY)] * 3,
            out_specs=pl.BlockSpec(memory_space=pl.ANY),
            scratch_shapes=[
                pltpu.VMEM(queries.shape, jnp.bfloat16),
                pltpu.VMEM((2,) + keys.shape, jnp.bfloat16),
                pltpu.VMEM((plane_rows, group * HEAD_DIM), jnp.bfloat16),
                pltpu.VMEM((2, total, HEAD_DIM), jnp.bfloat16),
                pltpu.VMEM((group * plane_rows, HEAD_DIM), jnp.float32),
                pltpu.VMEM((group * plane_rows, 2 * HEAD_DIM), jnp.float32),
                pltpu.VMEM((plane_rows, group * HEAD_DIM), jnp.bfloat16),
                dma((3,)),
                dma((4,)),
                pltpu.SemaphoreType.REGULAR,
                dma((members,)),
                dma((members,)),
                dma((members,)),
                dma((members,)),
                dma((members,)),
                dma((pieces,)),
                dma((pieces,)),
                dma((members,)),
                dma((members,)),
            ],
            compiler_params=pltpu.CompilerParams(collective_id=0, has_side_effects=True),
        )(queries, keys, values)

    spec = P(("seq", "head"), None)
    return jax.shard_map(
        on_device, mesh=mesh, in_specs=(spec, spec, spec), out_specs=spec, check_vma=False
    )
```

profile of v0, /device:TPU:24, one launch (start us, length us, event | category | flops | bytes accessed | tf_op | source)
XLA Modules:
  0.0 33.9 jit_solution(5283740700575297756)
XLA Ops:
  0.0 32.0 %shard_map.37 = bf16[64,4096]{1,0:T(8,128)(2,1)} custom-call(bf16[64,4096]{1,0:T(8,128)(2,1)} %q_in.1, bf16[64,1024]{1,0:T(8,128)(2,1)} %k_in.1, bf16[64,1024]{1,0:T(8,128)(2,1)} %v_in.1), custom_call_target="tpu_custom_call" | custom-call | tf_op jit(solution)/shard_map/pallas_call | solution.py:325
  32.0 1.9 %copy.5 = bf16[64,4096]{1,0:T(8,128)(2,1)} copy(bf16[64,4096]{1,0:T(8,128)(2,1)} %shard_map.37) | data formatting | bytes 1048576
where the time goes:
time: 34.1 us; the launch traced here: 33.9 us
  Pallas kernels  32 us (94%)
  local copies, waits for them, and re-layouts  1.87 us (5%)
    pallas_call x1, Pallas kernels, on_device(): pl.pallas_call(functools.partial(kernel, cfg), out_shape=jax.ShapeDtypeSt...  32 us
    unnamed x1, local copies, waits for them, and re-layouts  1.87 us

commit v1 on v0

--- a/solution.py
+++ b/solution.py
@@ -16,7 +16,7 @@
 
 def kernel(
     cfg, q_in, k_in, v_in, out_ref, q_stage, kv_stage, q_all, kv_all, largest, summed, result,
-    load_sem, own_sem, go_sem, kv_send, kv_recv, q_send, q_recv, rise_send, up_send, up_recv, out_send, out_recv,
+    load_sem, own_sem, kv_send, kv_recv, q_send, q_recv, rise_send, up_send, up_recv, out_send, out_recv,
 ):
     heads, planes, inner, group, rows, chunk = cfg
     members = heads * inner
@@ -33,13 +33,11 @@
     def member(g):
         return {"head": g % heads, "seq": plane * inner + g // heads}
 
-    def other_plane(step):
-        return {"head": head, "seq": seq + step * inner}
+    def other_plane(step, g=me):
+        return {"head": g % heads, "seq": (plane + step) * inner + g // heads}
 
     turns = inner % 2 == 0
     core = seq % 2 if turns else 0
-    first_turn = plane >= 0 if not turns else core == 0
-    second_turn = plane < 0 if not turns else core == 1
 
     def flip(mask, start=me):
         g, bit = start, 1
@@ -82,14 +80,16 @@
 
     @pl.when(has_up)
     def _():
-        pl.semaphore_signal(barrier, inc=1, device_id=other_plane(1), device_id_type=MESH)
+        for g in range(members):
+            pl.semaphore_signal(barrier, inc=1, device_id=other_plane(1, g), device_id_type=MESH)
 
     @pl.when(has_down)
     def _():
-        pl.semaphore_signal(barrier, inc=1, device_id=other_plane(-1), device_id_type=MESH)
+        for g in range(members):
+            pl.semaphore_signal(barrier, inc=1, device_id=other_plane(-1, g), device_id_type=MESH)
 
     beside = jnp.minimum(plane, 1) + jnp.minimum(planes - 1 - plane, 1)
-    pl.semaphore_wait(barrier, members - 1 + beside)
+    pl.semaphore_wait(barrier, members - 1 + beside * members)
 
     def kv_copy(src, dst, to):
         return pltpu.make_async_remote_copy(
@@ -121,13 +121,13 @@
             device_id_type=MESH,
         )
 
-    def rise_copy(src):
-        return pltpu.make_async_remote_copy(
-            src_ref=kv_all.at[:, position(src)],
-            dst_ref=kv_all.at[:, position(src)],
-            send_sem=rise_send.at[src],
-            recv_sem=up_recv.at[plane * chunks + src // (members // chunks)],
-            device_id=other_plane(1),
+    def rise_copy(dst):
+        return pltpu.make_async_remote_copy(
+            src_ref=kv_stage.at[:, :, cols(dst, HEAD_DIM)],
+            dst_ref=kv_all.at[:, position(me)],
+            send_sem=rise_send.at[dst],
+            recv_sem=up_recv.at[plane * chunks + me // (members // chunks)],
+            device_id=other_plane(1, dst),
             device_id_type=MESH,
         )
 
@@ -159,6 +159,12 @@
     loads[0].wait()
     loads[1].wait()
     start_all(kv_copy)
+
+    @pl.when(has_up)
+    def _():
+        for to in peers:
+            rise_copy(to).start()
+
     loads[2].wait()
     start_all(q_copy)
 
@@ -170,20 +176,6 @@
             own[0].wait()
             own[1].wait()
 
-        @pl.when(has_up & first_turn)
-        def _(src=src):
-            rise_copy(src).start()
-
-    def pass_turn(condition):
-        if turns:
-
-            @pl.when(has_up & first_turn & condition)
-            def _():
-                sibling = {"head": head, "seq": seq + 1}
-                pl.semaphore_signal(go_sem, inc=1, device_id=sibling, device_id_type=MESH)
-
-    pass_turn(plane <= 1)
-
     def receive(index):
         up_copy(index).wait_recv()
 
@@ -196,24 +188,14 @@
     def nearest(c):
         return (me // per_chunk + c) % chunks
 
-    if turns:
-
-        @pl.when(has_up & second_turn)
-        def _():
-            pl.semaphore_wait(go_sem, 1)
-            for mask in near_first:
-                rise_copy(flip(mask)).start()
-
     ahead = jnp.minimum(plane, 1)
     if turns:
-        ahead = jnp.where(first_turn, plane, ahead)
+        ahead = jnp.where(core == 0, plane, ahead)
     ahead = jnp.where(has_up, ahead, 0)
 
     def forward(step, carry):
         for c in range(chunks):
             receive((plane - step) * chunks + nearest(c))
-            if c == 0:
-                pass_turn(step == plane - 1)
         return carry
 
     lax.fori_loop(1, ahead + 1, forward, 0)
@@ -298,7 +280,7 @@
 
         lax.fori_loop(0, plane * chunks, sent, 0)
         for mask in range(members):
-            rise_copy(flip(mask)).wait_send()
+            rise_copy(mask).wait_send()
 
     for d in range(1, members):
         src = (me + d) % members
@@ -324,9 +306,9 @@
         cfg = (heads, planes, inner, group, rows, chunk)
         return pl.pallas_call(
             functools.partial(kernel, cfg),
-            out_shape=jax.ShapeDtypeStruct(queries.shape, jnp.bfloat16),
+            out_shape=pltpu.VMEM(queries.shape, jnp.bfloat16),
             in_specs=[pl.BlockSpec(memory_space=pl.ANY)] * 3,
-            out_specs=pl.BlockSpec(memory_space=pl.ANY),
+            out_specs=pl.BlockSpec(memory_space=pltpu.VMEM),
             scratch_shapes=[
                 pltpu.VMEM(queries.shape, jnp.bfloat16),
                 pltpu.VMEM((2,) + keys.shape, jnp.bfloat16),
@@ -337,7 +319,6 @@
                 pltpu.VMEM((plane_rows, group * HEAD_DIM), jnp.bfloat16),
                 dma((3,)),
                 dma((4,)),
-                pltpu.SemaphoreType.REGULAR,
                 dma((members,)),
                 dma((members,)),
                 dma((members,)),

time: 34.1 us -> 31.8 us (0.933)
  Pallas kernels: 32 us -> 30.9 us
  local copies, waits for them, and re-layouts: 1.87 us -> 0.8 us
    pallas_call x1, Pallas kernels: 32 us -> 30.9 us  [on_device(): pl.pallas_call(functools.partial(kernel, cfg), out_shape=pltpu.VMEM(queri...]
    unnamed x1, local copies, waits for them, and re-layouts: 1.87 us -> 0.8 us
where the time goes in v1:
time: 31.8 us; the launch traced here: 31.7 us
  Pallas kernels  30.9 us (97%)
  local copies, waits for them, and re-layouts  0.8 us (3%)
    pallas_call x1, Pallas kernels, on_device(): pl.pallas_call(functools.partial(kernel, cfg), out_shape=pltpu.VMEM(queri...  30.9 us
    unnamed x1, local copies, waits for them, and re-layouts  0.8 us

profile of v1, /device:TPU:24, one launch (start us, length us, event | category | flops | bytes accessed | tf_op | source)
XLA Modules:
  0.0 31.7 jit_solution(5046369146861518212)
XLA Ops:
  0.0 30.9 %shard_map.37 = bf16[64,4096]{1,0:T(8,128)(2,1)S(1)} custom-call(bf16[64,4096]{1,0:T(8,128)(2,1)} %q_in.1, bf16[64,1024]{1,0:T(8,128)(2,1)} %k_in.1, bf16[64,1024]{1,0:T(8,128)(2,1)} %v_in.1), custom_call_target="tpu_custom_call" | custom-call | tf_op jit(solution)/shard_map/pallas_call | solution.py:307
  30.9 0.8 %copy.5 = bf16[64,4096]{1,0:T(8,128)(2,1)} copy(bf16[64,4096]{1,0:T(8,128)(2,1)S(1)} %shard_map.37) | data formatting | bytes 1048576

commit v2 on v1

--- a/solution.py
+++ b/solution.py
@@ -141,16 +141,23 @@
             device_id_type=MESH,
         )
 
-    far_first = sorted(range(members), key=lambda m: (m < members // 2, m % 2, m))
-    near_first = sorted(range(members), key=lambda m: (m * chunks // members, m % 2, m))
-    if turns:
-        sends = sorted(far_first, key=lambda m: (m // heads) % 2)
-    else:
-        sends = far_first
-    peers = [flip(mask, me - core * heads) for mask in sends]
-
-    def start_all(copy_of):
-        for to in peers:
+    per_chunk = members // chunks
+    near = me // per_chunk
+    base = me - core * heads
+
+    def peer(mask):
+        return flip(mask, base)
+
+    def reach(mask):
+        g = mask // heads
+        return (mask % heads > 0) + 2 * (g // (2 if turns else 1) > 0)
+
+    core_of = {m: (m // heads) % 2 if turns else 0 for m in range(members)}
+    far_first = sorted(range(members), key=lambda m: (core_of[m], -reach(m), m))
+    near_first = sorted(range(members), key=lambda m: (core_of[m], reach(m), m))
+
+    def start_all(copy_of, order):
+        for to in map(peer, order):
 
             @pl.when(to != me)
             def _(to=to):
@@ -158,23 +165,15 @@
 
     loads[0].wait()
     loads[1].wait()
-    start_all(kv_copy)
+    start_all(kv_copy, far_first)
 
     @pl.when(has_up)
     def _():
-        for to in peers:
-            rise_copy(to).start()
+        for mask in far_first:
+            rise_copy(peer(mask)).start()
 
     loads[2].wait()
-    start_all(q_copy)
-
-    for mask in near_first:
-        src = flip(mask)
-        if mask:
-            kv_copy(src, me, src).wait_recv()
-        else:
-            own[0].wait()
-            own[1].wait()
+    start_all(q_copy, near_first)
 
     def receive(index):
         up_copy(index).wait_recv()
@@ -183,42 +182,36 @@
         def _():
             up_copy(index).start()
 
-    per_chunk = members // chunks
-
     def nearest(c):
-        return (me // per_chunk + c) % chunks
+        return (near + c) % chunks
+
+    def chunk_of(step, c):
+        return (plane - step) * chunks + nearest(c)
 
     ahead = jnp.minimum(plane, 1)
     if turns:
-        ahead = jnp.where(core == 0, plane, ahead)
+        ahead = plane
     ahead = jnp.where(has_up, ahead, 0)
 
     def forward(step, carry):
         for c in range(chunks):
-            receive((plane - step) * chunks + nearest(c))
+            receive(chunk_of(step, c))
         return carry
-
-    lax.fori_loop(1, ahead + 1, forward, 0)
-
-    own[2].wait()
-    for mask in range(1, members):
-        src = flip(mask)
-        q_copy(src, me, src).wait_recv()
 
     scale = math.log2(math.e) / math.sqrt(HEAD_DIM)
     ones = jnp.ones((chunk, HEAD_DIM), jnp.bfloat16)
 
-    def attend(index, tiles, first, masked):
+    def attend(index, tiles, first=False):
         keys = kv_all[0, piece(index), :]
         values = jnp.concatenate([kv_all[1, piece(index), :], ones], axis=1)
         for r in tiles:
             for j in range(group):
-                q = q_all[r * chunk:(r + 1) * chunk, j * HEAD_DIM:(j + 1) * HEAD_DIM]
-                at = slice(j * plane_rows + r * chunk, j * plane_rows + (r + 1) * chunk)
+                q = q_all[piece(r), j * HEAD_DIM:(j + 1) * HEAD_DIM]
+                at = pl.ds(pl.multiple_of(j * plane_rows + r * chunk, chunk), chunk)
                 score = lax.dot_general(
                     q, keys, (((1,), (1,)), ((), ())), preferred_element_type=jnp.float32
                 )
-                if r == masked:
+                if first:
                     row = lax.broadcasted_iota(jnp.int32, score.shape, 0)
                     col = lax.broadcasted_iota(jnp.int32, score.shape, 1)
                     score = jnp.where(col <= row, score, NEG)
@@ -236,21 +229,68 @@
                     summed[at, :] = summed[at, :] * jnp.concatenate([shrink, shrink], axis=1) + product
                 largest[at, :] = top
 
-    for c in range(chunks):
-        attend(plane * chunks + c, range(c, chunks), c == 0, c)
-
-    def earlier(step, carry):
-        for c in range(chunks):
-            index = (plane - step) * chunks + nearest(c)
+    def kv_ready(mask):
+        src = flip(mask)
+        if mask:
+            kv_copy(src, me, src).wait_recv()
+        else:
+            own[0].wait()
+            own[1].wait()
+
+    def q_ready(mask):
+        src = flip(mask)
+        if mask:
+            q_copy(src, me, src).wait_recv()
+        else:
+            own[2].wait()
+
+    def own_tile(shift):
+        r = nearest(shift)
+        attend(plane * chunks + r, [r], first=True)
+        for c in range(chunks - 1):
+
+            @pl.when(c < r)
+            def _(c=c):
+                attend(plane * chunks + c, [r])
+
+    lax.fori_loop(1, ahead + 1, forward, 0)
+
+    for mask in range(members):
+        kv_ready(mask)
+    for mask in range(per_chunk):
+        q_ready(mask)
+    own_tile(0)
+
+    for mask in range(per_chunk, members):
+        q_ready(mask)
+    for shift in range(1, chunks):
+        own_tile(shift)
+
+    def earlier(step, count):
+        for c in range(count):
+            index = chunk_of(step, c)
 
             @pl.when(step > ahead)
             def _():
                 receive(index)
 
-            attend(index, range(chunks), False, -1)
+            attend(index, range(chunks))
+
+    def whole_step(step, carry):
+        earlier(step, chunks)
         return carry
 
-    lax.fori_loop(1, plane + 1, earlier, 0)
+    lax.fori_loop(1, plane, whole_step, 0)
+
+    final = chunk_of(plane, chunks - 1)
+
+    @pl.when(has_down)
+    def _():
+        earlier(plane, chunks - 1)
+
+        @pl.when(plane > ahead)
+        def _():
+            receive(final)
 
     def finish(g):
         for j in range(group):
@@ -259,11 +299,18 @@
                 summed[at, :HEAD_DIM] / summed[at, HEAD_DIM:]
             ).astype(jnp.bfloat16)
 
-    for mask in far_first:
-        to = flip(mask)
-        finish(to)
-        if mask:
-            out_copy(me, to, to).start()
+    for shift in reversed(range(chunks)):
+
+        @pl.when(has_down)
+        def _(shift=shift):
+            attend(final, [nearest(shift)])
+
+        tile = range(shift * per_chunk, (shift + 1) * per_chunk)
+        for mask in sorted(tile, key=lambda m: (-reach(m), m)):
+            to = flip(mask)
+            finish(to)
+            if mask:
+                out_copy(me, to, to).start()
     keep = pltpu.make_async_copy(result.at[block(me)], out_ref.at[:, cols(me, width)], own_sem.at[3])
     keep.start()
 

time: 31.8 us -> 30.6 us (0.962)
  the two profiles are of different devices: /device:TPU:24 before, /device:TPU:25 now
where the time goes in v2:
time: 30.6 us; the launch traced here: 30.3 us
  Pallas kernels  29.5 us (96%)
  local copies, waits for them, and re-layouts  0.8 us (3%)
    pallas_call x1, Pallas kernels, on_device(): pl.pallas_call(functools.partial(kernel, cfg), out_shape=pltpu.VMEM(queri...  29.5 us
    unnamed x1, local copies, waits for them, and re-layouts  0.8 us

profile of v2, /device:TPU:25, one launch (start us, length us, event | category | flops | bytes accessed | tf_op | source)
XLA Modules:
  0.0 30.3 jit_solution(6383250617305821417)
XLA Ops:
  0.0 29.5 %shard_map.37 = bf16[64,4096]{1,0:T(8,128)(2,1)S(1)} custom-call(bf16[64,4096]{1,0:T(8,128)(2,1)} %q_in.1, bf16[64,1024]{1,0:T(8,128)(2,1)} %k_in.1, bf16[64,1024]{1,0:T(8,128)(2,1)} %v_in.1), custom_call_target="tpu_custom_call" | custom-call | tf_op jit(solution)/shard_map/pallas_call | solution.py:354
  29.5 0.8 %copy.5 = bf16[64,4096]{1,0:T(8,128)(2,1)} copy(bf16[64,4096]{1,0:T(8,128)(2,1)S(1)} %shard_map.37) | data formatting | bytes 1048576

commit v3 on v2

--- a/solution.py
+++ b/solution.py
@@ -16,7 +16,7 @@
 
 def kernel(
     cfg, q_in, k_in, v_in, out_ref, q_stage, kv_stage, q_all, kv_all, largest, summed, result,
-    load_sem, own_sem, kv_send, kv_recv, q_send, q_recv, rise_send, up_send, up_recv, out_send, out_recv,
+    load_sem, own_sem, go_sem, kv_send, kv_recv, q_send, q_recv, rise_send, up_send, up_recv, out_send, out_recv,
 ):
     heads, planes, inner, group, rows, chunk = cfg
     members = heads * inner
@@ -78,18 +78,13 @@
             barrier, inc=1, device_id=member((me + d) % members), device_id_type=MESH
         )
 
-    @pl.when(has_up)
-    def _():
-        for g in range(members):
-            pl.semaphore_signal(barrier, inc=1, device_id=other_plane(1, g), device_id_type=MESH)
-
     @pl.when(has_down)
     def _():
         for g in range(members):
             pl.semaphore_signal(barrier, inc=1, device_id=other_plane(-1, g), device_id_type=MESH)
 
-    beside = jnp.minimum(plane, 1) + jnp.minimum(planes - 1 - plane, 1)
-    pl.semaphore_wait(barrier, members - 1 + beside * members)
+    above = jnp.minimum(planes - 1 - plane, 1)
+    pl.semaphore_wait(barrier, members - 1 + above * members)
 
     def kv_copy(src, dst, to):
         return pltpu.make_async_remote_copy(
@@ -163,17 +158,19 @@
             def _(to=to):
                 copy_of(me, to, to).start()
 
-    loads[0].wait()
-    loads[1].wait()
-    start_all(kv_copy, far_first)
-
-    @pl.when(has_up)
-    def _():
-        for mask in far_first:
-            rise_copy(peer(mask)).start()
-
-    loads[2].wait()
-    start_all(q_copy, near_first)
+    for load in loads:
+        load.wait()
+
+    for side in range(1 + max(core_of.values())):
+        start_all(kv_copy, [m for m in far_first if core_of[m] == side])
+
+        @pl.when(has_up)
+        def _(side=side):
+            for mask in far_first:
+                if core_of[mask] == side:
+                    rise_copy(peer(mask)).start()
+
+        start_all(q_copy, [m for m in near_first if core_of[m] == side])
 
     def receive(index):
         up_copy(index).wait_recv()
@@ -193,8 +190,19 @@
         ahead = plane
     ahead = jnp.where(has_up, ahead, 0)
 
+    waits = has_up & (plane > 1)
+
+    def hold(at):
+        if turns:
+
+            @pl.when(waits & (core == 1) & at)
+            def _():
+                pl.semaphore_wait(go_sem, 1)
+
     def forward(step, carry):
         for c in range(chunks):
+            if c == 1:
+                hold(step == 1)
             receive(chunk_of(step, c))
         return carry
 
@@ -255,6 +263,13 @@
 
     lax.fori_loop(1, ahead + 1, forward, 0)
 
+    if turns:
+
+        @pl.when(waits & (core == 0))
+        def _():
+            sibling = {"head": head, "seq": seq + 1}
+            pl.semaphore_signal(go_sem, inc=1, device_id=sibling, device_id_type=MESH)
+
     for mask in range(members):
         kv_ready(mask)
     for mask in range(per_chunk):
@@ -366,6 +381,7 @@
                 pltpu.VMEM((plane_rows, group * HEAD_DIM), jnp.bfloat16),
                 dma((3,)),
                 dma((4,)),
+                pltpu.SemaphoreType.REGULAR,
                 dma((members,)),
                 dma((members,)),
                 dma((members,)),

time: 30.6 us -> 29.8 us (0.974)
  the two profiles are of different devices: /device:TPU:25 before, /device:TPU:21 now
where the time goes in v3:
time: 29.8 us; the launch traced here: 29.6 us
  Pallas kernels  28.8 us (97%)
  local copies, waits for them, and re-layouts  0.8 us (3%)
    pallas_call x1, Pallas kernels, on_device(): pl.pallas_call(functools.partial(kernel, cfg), out_shape=pltpu.VMEM(queri...  28.8 us
    unnamed x1, local copies, waits for them, and re-layouts  0.8 us

profile of v3, /device:TPU:21, one launch (start us, length us, event | category | flops | bytes accessed | tf_op | source)
XLA Modules:
  0.0 29.6 jit_solution(10604154433136876115)
XLA Ops:
  0.0 28.8 %shard_map.37 = bf16[64,4096]{1,0:T(8,128)(2,1)S(1)} custom-call(bf16[64,4096]{1,0:T(8,128)(2,1)} %q_in.1, bf16[64,1024]{1,0:T(8,128)(2,1)} %k_in.1, bf16[64,1024]{1,0:T(8,128)(2,1)} %v_in.1), custom_call_target="tpu_custom_call" | custom-call | tf_op jit(solution)/shard_map/pallas_call | solution.py:369
  28.8 0.8 %copy.5 = bf16[64,4096]{1,0:T(8,128)(2,1)} copy(bf16[64,4096]{1,0:T(8,128)(2,1)S(1)} %shard_map.37) | data formatting | bytes 1048576

commit v4 on v3

--- a/solution.py
+++ b/solution.py
@@ -190,21 +190,25 @@
         ahead = plane
     ahead = jnp.where(has_up, ahead, 0)
 
-    waits = has_up & (plane > 1)
-
-    def hold(at):
-        if turns:
-
-            @pl.when(waits & (core == 1) & at)
-            def _():
-                pl.semaphore_wait(go_sem, 1)
-
     def forward(step, carry):
         for c in range(chunks):
-            if c == 1:
-                hold(step == 1)
             receive(chunk_of(step, c))
         return carry
+
+    relays = has_up & has_down
+    leads = relays & (core == 0) & turns
+    trails = relays & (core == 1) & turns
+
+    def lead_sent(first, last):
+        for c in range(first, last):
+            up_copy(chunk_of(plane, c)).wait_send()
+
+    def pass_turn():
+        sibling = {"head": head, "seq": seq + 1}
+        pl.semaphore_signal(go_sem, inc=1, device_id=sibling, device_id_type=MESH)
+
+    def take_turn():
+        pl.semaphore_wait(go_sem, 1)
 
     scale = math.log2(math.e) / math.sqrt(HEAD_DIM)
     ones = jnp.ones((chunk, HEAD_DIM), jnp.bfloat16)
@@ -261,14 +265,30 @@
             def _(c=c):
                 attend(plane * chunks + c, [r])
 
-    lax.fori_loop(1, ahead + 1, forward, 0)
-
     if turns:
 
-        @pl.when(waits & (core == 0))
-        def _():
-            sibling = {"head": head, "seq": seq + 1}
-            pl.semaphore_signal(go_sem, inc=1, device_id=sibling, device_id_type=MESH)
+        @pl.when(leads)
+        def _():
+            lax.fori_loop(1, plane + 1, forward, 0)
+
+            @pl.when(plane == 1)
+            def _():
+                lead_sent(0, chunks)
+                pass_turn()
+
+        @pl.when(trails)
+        def _():
+            @pl.when(plane == 1)
+            def _():
+                take_turn()
+                forward(1, 0)
+
+            @pl.when(plane > 1)
+            def _():
+                receive(chunk_of(1, 0))
+
+    else:
+        lax.fori_loop(1, ahead + 1, forward, 0)
 
     for mask in range(members):
         kv_ready(mask)
@@ -276,10 +296,32 @@
         q_ready(mask)
     own_tile(0)
 
+    if turns:
+
+        @pl.when(trails & (plane > 1))
+        def _():
+            take_turn()
+            for c in range(1, chunks):
+                receive(chunk_of(1, c))
+            lax.fori_loop(2, plane, forward, 0)
+            for c in range(chunks - 1):
+                receive(chunk_of(plane, c))
+
     for mask in range(per_chunk, members):
         q_ready(mask)
     for shift in range(1, chunks):
         own_tile(shift)
+
+    if turns:
+
+        @pl.when(leads & (plane > 1))
+        def _():
+            lead_sent(0, 1)
+            pass_turn()
+
+        @pl.when(trails & (plane > 1))
+        def _():
+            receive(chunk_of(plane, chunks - 1))
 
     def earlier(step, count):
         for c in range(count):
@@ -337,10 +379,14 @@
     @pl.when(has_up)
     def _():
         def sent(index, carry):
-            up_copy(index).wait_send()
+            @pl.when((index != chunk_of(plane, 0)) | jnp.logical_not(leads & (plane > 1)))
+            def _():
+                up_copy(index).wait_send()
+
             return carry
 
-        lax.fori_loop(0, plane * chunks, sent, 0)
+        done = jnp.where(leads & (plane == 1), chunks, 0) if turns else 0
+        lax.fori_loop(done, plane * chunks, sent, 0)
         for mask in range(members):
             rise_copy(mask).wait_send()
 

time: 29.8 us -> 29 us (0.973)
  the two profiles are of different devices: /device:TPU:21 before, /device:TPU:25 now
where the time goes in v4:
time: 29 us; the launch traced here: 28.5 us
  Pallas kernels  27.7 us (96%)
  local copies, waits for them, and re-layouts  0.8 us (3%)
    pallas_call x1, Pallas kernels, on_device(): pl.pallas_call(functools.partial(kernel, cfg), out_shape=pltpu.VMEM(queri...  27.7 us
    unnamed x1, local copies, waits for them, and re-layouts  0.8 us

profile of v4, /device:TPU:25, one launch (start us, length us, event | category | flops | bytes accessed | tf_op | source)
XLA Modules:
  0.0 28.5 jit_solution(1546538897594230604)
XLA Ops:
  0.0 27.7 %shard_map.37 = bf16[64,4096]{1,0:T(8,128)(2,1)S(1)} custom-call(bf16[64,4096]{1,0:T(8,128)(2,1)} %q_in.1, bf16[64,1024]{1,0:T(8,128)(2,1)} %k_in.1, bf16[64,1024]{1,0:T(8,128)(2,1)} %v_in.1), custom_call_target="tpu_custom_call" | custom-call | tf_op jit(solution)/shard_map/pallas_call | solution.py:415
  27.7 0.8 %copy.5 = bf16[64,4096]{1,0:T(8,128)(2,1)} copy(bf16[64,4096]{1,0:T(8,128)(2,1)S(1)} %shard_map.37) | data formatting | bytes 1048576

commit v5 on v4

v5 whole, which is shorter than its diff:
```python
import functools
import math

import jax
import jax.numpy as jnp
from jax import lax
from jax.experimental import pallas as pl
from jax.experimental.pallas import tpu as pltpu
from jax.sharding import PartitionSpec as P

HEAD_DIM = 128
TILE = 256
MESH = pl.DeviceIdType.MESH
NEG = -1e30


def kernel(
    cfg, q_in, k_in, v_in, out_ref, q_stage, kv_stage, q_all, kv_all, largest, summed, result,
    load_sem, go_sem, kv_send, kv_recv, q_send, q_recv, rise_send, up_send, up_recv, out_send, out_recv,
):
    heads, planes, inner, group, rows, chunk = cfg
    members = heads * inner
    plane_rows = members * rows
    chunks = plane_rows // chunk
    per_chunk = members // chunks
    width = group * HEAD_DIM
    seq = lax.axis_index("seq")
    head = lax.axis_index("head")
    plane = seq // inner
    me = (seq % inner) * heads + head
    near = me // per_chunk
    has_up = plane < planes - 1
    has_down = plane > 0

    def member(g):
        return {"head": g % heads, "seq": plane * inner + g // heads}

    def other_plane(step, g=me):
        return {"head": g % heads, "seq": (plane + step) * inner + g // heads}

    turns = inner % 2 == 0
    core = seq % 2 if turns else 0

    def flip(mask, start=me):
        g, bit = start, 1
        while bit < members:
            if mask & bit:
                g = g + bit * (1 - 2 * ((start // bit) % 2))
            bit *= 2
        return g

    def cols(g, size):
        return pl.ds(pl.multiple_of(g * size, HEAD_DIM), size)

    def block(g):
        return pl.ds(pl.multiple_of(g * rows, rows), rows)

    def position(g):
        return pl.ds(pl.multiple_of((plane * members + g) * rows, rows), rows)

    def plane_of(index):
        return pl.ds(pl.multiple_of(index * plane_rows, plane_rows), plane_rows)

    def piece(index):
        return pl.ds(pl.multiple_of(index * chunk, chunk), chunk)

    loads = [
        pltpu.make_async_copy(k_in, kv_stage.at[0], load_sem.at[0]),
        pltpu.make_async_copy(v_in, kv_stage.at[1], load_sem.at[0]),
        pltpu.make_async_copy(q_in, q_stage, load_sem.at[1]),
    ]
    own = [
        pltpu.make_async_copy(k_in.at[:, cols(me, HEAD_DIM)], kv_all.at[0, position(me)], kv_recv),
        pltpu.make_async_copy(v_in.at[:, cols(me, HEAD_DIM)], kv_all.at[1, position(me)], kv_recv),
        pltpu.make_async_copy(q_in.at[:, cols(me, width)], q_all.at[block(me)], q_recv.at[near]),
    ]
    for copy in loads + own:
        copy.start()

    barrier = pltpu.get_barrier_semaphore()
    for d in range(1, members):
        pl.semaphore_signal(
            barrier, inc=1, device_id=member((me + d) % members), device_id_type=MESH
        )

    @pl.when(has_down)
    def _():
        for g in range(members):
            pl.semaphore_signal(barrier, inc=1, device_id=other_plane(-1, g), device_id_type=MESH)

    above = jnp.minimum(planes - 1 - plane, 1)
    pl.semaphore_wait(barrier, members - 1 + above * members)

    def kv_copy(src, dst, to):
        return pltpu.make_async_remote_copy(
            src_ref=kv_stage.at[:, :, cols(dst, HEAD_DIM)],
            dst_ref=kv_all.at[:, position(src)],
            send_sem=kv_send,
            recv_sem=kv_recv,
            device_id=member(to),
            device_id_type=MESH,
        )

    def q_copy(src, dst, to):
        return pltpu.make_async_remote_copy(
            src_ref=q_stage.at[:, cols(dst, width)],
            dst_ref=q_all.at[block(src)],
            send_sem=q_send,
            recv_sem=q_recv.at[src // per_chunk],
            device_id=member(to),
            device_id_type=MESH,
        )

    def up_copy(index):
        return pltpu.make_async_remote_copy(
            src_ref=kv_all.at[:, piece(index)],
            dst_ref=kv_all.at[:, piece(index)],
            send_sem=up_send.at[index],
            recv_sem=up_recv.at[index],
            device_id=other_plane(1),
            device_id_type=MESH,
        )

    def rise_copy(dst):
        return pltpu.make_async_remote_copy(
            src_ref=kv_stage.at[:, :, cols(dst, HEAD_DIM)],
            dst_ref=kv_all.at[:, position(me)],
            send_sem=rise_send,
            recv_sem=up_recv.at[plane * chunks + near],
            device_id=other_plane(1, dst),
            device_id_type=MESH,
        )

    def out_copy(src, dst, to):
        return pltpu.make_async_remote_copy(
            src_ref=result.at[block(dst)],
            dst_ref=out_ref.at[:, cols(src, width)],
            send_sem=out_send,
            recv_sem=out_recv,
            device_id=member(to),
            device_id_type=MESH,
        )

    base = me - core * heads

    def peer(mask):
        return flip(mask, base)

    def reach(mask):
        g = mask // heads
        return (mask % heads > 0) + 2 * (g // (2 if turns else 1) > 0)

    core_of = {m: (m // heads) % 2 if turns else 0 for m in range(members)}
    far_first = sorted(range(members), key=lambda m: (core_of[m], -reach(m), m))
    near_first = sorted(range(members), key=lambda m: (core_of[m], reach(m), m))

    def start_all(copy_of, order):
        for to in map(peer, order):

            @pl.when(to != me)
            def _(to=to):
                copy_of(me, to, to).start()

    def wait_all(ref, sem):
        pltpu.make_async_copy(ref, ref, sem).wait()

    wait_all(kv_stage, load_sem.at[0])
    wait_all(q_stage, load_sem.at[1])

    for side in range(1 + max(core_of.values())):
        start_all(kv_copy, [m for m in far_first if core_of[m] == side])

        @pl.when(has_up)
        def _(side=side):
            for mask in far_first:
                if core_of[mask] == side:
                    rise_copy(peer(mask)).start()

        start_all(q_copy, [m for m in near_first if core_of[m] == side])

    def receive(index):
        wait_all(kv_all.at[:, piece(index)], up_recv.at[index])

        @pl.when(has_up)
        def _():
            up_copy(index).start()

    def nearest(c):
        return (near + c) % chunks

    def chunk_of(step, c):
        return (plane - step) * chunks + nearest(c)

    ahead = jnp.minimum(plane, 1)
    if turns:
        ahead = plane
    ahead = jnp.where(has_up, ahead, 0)

    def forward(step, carry):
        for c in range(chunks):
            receive(chunk_of(step, c))
        return carry

    relays = has_up & has_down
    leads = relays & (core == 0) & turns
    trails = relays & (core == 1) & turns

    def lead_sent(first, last):
        for c in range(first, last):
            up_copy(chunk_of(plane, c)).wait_send()

    def pass_turn():
        sibling = {"head": head, "seq": seq + 1}
        pl.semaphore_signal(go_sem, inc=1, device_id=sibling, device_id_type=MESH)

    def take_turn():
        pl.semaphore_wait(go_sem, 1)

    scale = math.log2(math.e) / math.sqrt(HEAD_DIM)
    sub = chunk // 2 if chunk >= 2 * HEAD_DIM else chunk
    per_sub = sub // rows

    def attend(at_keys, row0, size, first=False):
        keys = kv_all[0, at_keys, :]
        count = keys.shape[0]
        ones = jnp.ones((count, HEAD_DIM), jnp.bfloat16)
        values = jnp.concatenate([kv_all[1, at_keys, :], ones], axis=1)
        for j in range(group):
            q = q_all[pl.ds(pl.multiple_of(row0, size), size), j * HEAD_DIM:(j + 1) * HEAD_DIM]
            at = pl.ds(pl.multiple_of(j * plane_rows + row0, size), size)
            score = lax.dot_general(
                q, keys, (((1,), (1,)), ((), ())), preferred_element_type=jnp.float32
            )
            if first:
                row = lax.broadcasted_iota(jnp.int32, score.shape, 0) + (count - size)
                col = lax.broadcasted_iota(jnp.int32, score.shape, 1)
                score = jnp.where(col <= row, score, NEG)
            top = jnp.broadcast_to(jnp.max(score, axis=1, keepdims=True), (size, HEAD_DIM))
            if not first:
                before = largest[at, :]
                top = jnp.maximum(before, top)
            spread = jnp.concatenate([top] * (count // HEAD_DIM), axis=1)
            weight = jnp.exp2((score - spread) * scale).astype(jnp.bfloat16)
            product = jnp.dot(weight, values, preferred_element_type=jnp.float32)
            if first:
                summed[at, :] = product
            else:
                shrink = jnp.exp2((before - top) * scale)
                summed[at, :] = summed[at, :] * jnp.concatenate([shrink, shrink], axis=1) + product
            largest[at, :] = top

    def own_tile(shift):
        for r in range(chunks):

            @pl.when(nearest(shift) == r)
            def _(r=r):
                at_keys = pl.ds(pl.multiple_of(plane * plane_rows, plane_rows), (r + 1) * chunk)
                attend(at_keys, r * chunk, chunk, first=True)

    if turns:

        @pl.when(leads)
        def _():
            lax.fori_loop(1, plane + 1, forward, 0)

            @pl.when(plane == 1)
            def _():
                lead_sent(0, chunks)
                pass_turn()

        @pl.when(trails)
        def _():
            @pl.when(plane == 1)
            def _():
                take_turn()
                forward(1, 0)

            @pl.when(plane > 1)
            def _():
                receive(chunk_of(1, 0))

    else:
        lax.fori_loop(1, ahead + 1, forward, 0)

    wait_all(kv_all.at[:, plane_of(plane)], kv_recv)
    wait_all(q_all.at[piece(near)], q_recv.at[near])
    own_tile(0)

    if turns:

        @pl.when(trails & (plane > 1))
        def _():
            take_turn()
            for c in range(1, chunks):
                receive(chunk_of(1, c))
            lax.fori_loop(2, plane, forward, 0)
            for c in range(chunks - 1):
                receive(chunk_of(plane, c))

    for shift in range(1, chunks):
        wait_all(q_all.at[piece(nearest(shift))], q_recv.at[nearest(shift)])
        own_tile(shift)

    if turns:

        @pl.when(leads & (plane > 1))
        def _():
            lead_sent(0, 1)
            pass_turn()

        @pl.when(trails & (plane > 1))
        def _():
            receive(chunk_of(plane, chunks - 1))

    def arrive(step, c):
        @pl.when(step > ahead)
        def _():
            receive(chunk_of(step, c))

    def whole_step(step, carry):
        for c in range(chunks):
            arrive(step, c)
        for row0 in range(0, plane_rows, chunk):
            attend(plane_of(plane - step), row0, chunk)
        return carry

    lax.fori_loop(1, plane, whole_step, 0)

    final = piece(chunk_of(plane, chunks - 1))

    @pl.when(has_down)
    def _():
        for c in range(chunks - 1):
            arrive(plane, c)
            for r in range(chunks):
                attend(piece(chunk_of(plane, c)), r * chunk, chunk)
        arrive(plane, chunks - 1)

    def finish(g):
        for j in range(group):
            at = pl.ds(pl.multiple_of(j * plane_rows + g * rows, rows), rows)
            result[block(g), j * HEAD_DIM:(j + 1) * HEAD_DIM] = (
                summed[at, :HEAD_DIM] / summed[at, HEAD_DIM:]
            ).astype(jnp.bfloat16)

    def close(attending):
        for shift in reversed(range(chunks)):
            for s in range(0, chunk, sub):
                row0 = nearest(shift) * chunk + s
                if attending:
                    attend(final, row0, sub)
                for i in range(per_sub):
                    to = row0 // rows + (me + 1 + i) % per_sub
                    finish(to)

                    @pl.when(to != me)
                    def _(to=to):
                        out_copy(me, to, to).start()

    @pl.when(has_down)
    def _():
        close(True)

    @pl.when(plane == 0)
    def _():
        close(False)

    pltpu.make_async_copy(result.at[block(me)], out_ref.at[:, cols(me, width)], out_recv).start()

    others = (members - 1) * HEAD_DIM
    kv_sent = kv_stage.at[:, :, :others]
    q_sent = q_stage.at[:, :group * others]
    wait_all(kv_sent, kv_send)
    wait_all(q_sent, q_send)

    @pl.when(has_up)
    def _():
        def sent(index, carry):
            @pl.when((index != chunk_of(plane, 0)) | jnp.logical_not(leads & (plane > 1)))
            def _():
                up_copy(index).wait_send()

            return carry

        done = jnp.where(leads & (plane == 1), chunks, 0) if turns else 0
        lax.fori_loop(done, plane * chunks, sent, 0)
        wait_all(kv_stage, rise_send)

    wait_all(result.at[:(members - 1) * rows], out_send)
    wait_all(out_ref, out_recv)


def solution(mesh):
    heads, seqs = mesh.shape["head"], mesh.shape["seq"]

    def on_device(queries, keys, values):
        rows = queries.shape[0]
        members = keys.shape[1] // HEAD_DIM
        inner = members // heads
        planes = seqs // inner
        group = queries.shape[1] // keys.shape[1]
        plane_rows = members * rows
        chunk = math.gcd(plane_rows, TILE)
        total = planes * plane_rows
        chunks = plane_rows // chunk
        relayed = max(planes - 2, 1) * chunks
        raised = max(planes - 1, 1) * chunks
        dma = pltpu.SemaphoreType.DMA
        cfg = (heads, planes, inner, group, rows, chunk)
        return pl.pallas_call(
            functools.partial(kernel, cfg),
            out_shape=pltpu.VMEM(queries.shape, jnp.bfloat16),
            in_specs=[pl.BlockSpec(memory_space=pl.ANY)] * 3,
            out_specs=pl.BlockSpec(memory_space=pltpu.VMEM),
            scratch_shapes=[
                pltpu.VMEM(queries.shape, jnp.bfloat16),
                pltpu.VMEM((2,) + keys.shape, jnp.bfloat16),
                pltpu.VMEM((plane_rows, group * HEAD_DIM), jnp.bfloat16),
                pltpu.VMEM((2, total, HEAD_DIM), jnp.bfloat16),
                pltpu.VMEM((group * plane_rows, HEAD_DIM), jnp.float32),
                pltpu.VMEM((group * plane_rows, 2 * HEAD_DIM), jnp.float32),
                pltpu.VMEM((plane_rows, group * HEAD_DIM), jnp.bfloat16),
                dma((2,)),
                pltpu.SemaphoreType.REGULAR,
                dma(()),
                dma(()),
                dma(()),
                dma((chunks,)),
                dma(()),
                dma((relayed,)),
                dma((raised,)),
                dma(()),
                dma(()),
            ],
            compiler_params=pltpu.CompilerParams(collective_id=0, has_side_effects=True),
        )(queries, keys, values)

    spec = P(("seq", "head"), None)
    return jax.shard_map(
        on_device, mesh=mesh, in_specs=(spec, spec, spec), out_specs=spec, check_vma=False
    )
```

time: 29 us -> 28.2 us (0.972); the launches traced: 28.5 us -> 28.1 us
  Pallas kernels: 27.7 us -> 27.3 us
    pallas_call x1, Pallas kernels: 27.7 us -> 27.3 us  [on_device(): pl.pallas_call(functools.partial(kernel, cfg), out_shape=pltpu.VMEM(queri...]
where the time goes in v5:
time: 28.2 us; the launch traced here: 28.1 us
  Pallas kernels  27.3 us (97%)
  local copies, waits for them, and re-layouts  0.8 us (3%)
    pallas_call x1, Pallas kernels, on_device(): pl.pallas_call(functools.partial(kernel, cfg), out_shape=pltpu.VMEM(queri...  27.3 us
    unnamed x1, local copies, waits for them, and re-layouts  0.8 us

profile of v5, /device:TPU:25, one launch (start us, length us, event | category | flops | bytes accessed | tf_op | source)
XLA Modules:
  0.0 28.1 jit_solution(2455724539509786047)
XLA Ops:
  0.0 27.3 %shard_map.37 = bf16[64,4096]{1,0:T(8,128)(2,1)S(1)} custom-call(bf16[64,4096]{1,0:T(8,128)(2,1)} %q_in.1, bf16[64,1024]{1,0:T(8,128)(2,1)} %k_in.1, bf16[64,1024]{1,0:T(8,128)(2,1)} %v_in.1), custom_call_target="tpu_custom_call" | custom-call | tf_op jit(solution)/shard_map/pallas_call | solution.py:410
  27.3 0.8 %copy.5 = bf16[64,4096]{1,0:T(8,128)(2,1)} copy(bf16[64,4096]{1,0:T(8,128)(2,1)S(1)} %shard_map.37) | data formatting | bytes 1048576

commit v6 on v5

--- a/solution.py
+++ b/solution.py
@@ -345,13 +345,17 @@
 
     def close(attending):
         for shift in reversed(range(chunks)):
-            for s in range(0, chunk, sub):
+            size = chunk if shift else chunk
+            for s in range(0, chunk, size):
                 row0 = nearest(shift) * chunk + s
                 if attending:
-                    attend(final, row0, sub)
-                for i in range(per_sub):
-                    to = row0 // rows + (me + 1 + i) % per_sub
+                    attend(final, row0, size)
+                for i in range(size // rows):
+                    to = row0 // rows + (me + 1 + i) % (size // rows)
                     finish(to)
+                    if shift:
+                        out_copy(me, to, to).start()
+                        continue
 
                     @pl.when(to != me)
                     def _(to=to):

time: 28.2 us -> 28 us (level)
  Pallas kernels: 27.3 us -> 27 us
where the time goes in v6:
time: 28 us; the launch traced here: 27.8 us
  Pallas kernels  27 us (96%)
  local copies, waits for them, and re-layouts  0.8 us (3%)
    pallas_call x1, Pallas kernels, on_device(): pl.pallas_call(functools.partial(kernel, cfg), out_shape=pltpu.VMEM(queri...  27 us
    unnamed x1, local copies, waits for them, and re-layouts  0.8 us

profile of v6, /device:TPU:25, one launch (start us, length us, event | category | flops | bytes accessed | tf_op | source)
XLA Modules:
  0.0 27.8 jit_solution(4383068321552766692)
XLA Ops:
  0.0 27.0 %shard_map.37 = bf16[64,4096]{1,0:T(8,128)(2,1)S(1)} custom-call(bf16[64,4096]{1,0:T(8,128)(2,1)} %q_in.1, bf16[64,1024]{1,0:T(8,128)(2,1)} %k_in.1, bf16[64,1024]{1,0:T(8,128)(2,1)} %v_in.1), custom_call_target="tpu_custom_call" | custom-call | tf_op jit(solution)/shard_map/pallas_call | solution.py:414
  27.0 0.8 %copy.5 = bf16[64,4096]{1,0:T(8,128)(2,1)} copy(bf16[64,4096]{1,0:T(8,128)(2,1)S(1)} %shard_map.37) | data formatting | bytes 1048576

commit v7 on v6

--- a/solution.py
+++ b/solution.py
@@ -74,19 +74,19 @@
         pltpu.make_async_copy(v_in.at[:, cols(me, HEAD_DIM)], kv_all.at[1, position(me)], kv_recv),
         pltpu.make_async_copy(q_in.at[:, cols(me, width)], q_all.at[block(me)], q_recv.at[near]),
     ]
-    for copy in loads + own:
-        copy.start()
-
     barrier = pltpu.get_barrier_semaphore()
-    for d in range(1, members):
-        pl.semaphore_signal(
-            barrier, inc=1, device_id=member((me + d) % members), device_id_type=MESH
-        )
-
     @pl.when(has_down)
     def _():
         for g in range(members):
             pl.semaphore_signal(barrier, inc=1, device_id=other_plane(-1, g), device_id_type=MESH)
+
+    for d in range(1, members):
+        pl.semaphore_signal(
+            barrier, inc=1, device_id=member((me + d) % members), device_id_type=MESH
+        )
+
+    for copy in loads + own:
+        copy.start()
 
     above = jnp.minimum(planes - 1 - plane, 1)
     pl.semaphore_wait(barrier, members - 1 + above * members)

time: 28 us -> 27.9 us (level)
  no operation moved by 1% of the time
where the time goes in v7:
time: 27.9 us; the launch traced here: 27.7 us
  Pallas kernels  26.9 us (96%)
  local copies, waits for them, and re-layouts  0.8 us (3%)
    pallas_call x1, Pallas kernels, on_device(): pl.pallas_call(functools.partial(kernel, cfg), out_shape=pltpu.VMEM(queri...  26.9 us
    unnamed x1, local copies, waits for them, and re-layouts  0.8 us

profile of v7, /device:TPU:25, one launch (start us, length us, event | category | flops | bytes accessed | tf_op | source)
XLA Modules:
  0.0 27.7 jit_solution(6509329376804420527)
XLA Ops:
  0.0 26.9 %shard_map.37 = bf16[64,4096]{1,0:T(8,128)(2,1)S(1)} custom-call(bf16[64,4096]{1,0:T(8,128)(2,1)} %q_in.1, bf16[64,1024]{1,0:T(8,128)(2,1)} %k_in.1, bf16[64,1024]{1,0:T(8,128)(2,1)} %v_in.1), custom_call_target="tpu_custom_call" | custom-call | tf_op jit(solution)/shard_map/pallas_call | solution.py:414
  26.9 0.8 %copy.5 = bf16[64,4096]{1,0:T(8,128)(2,1)} copy(bf16[64,4096]{1,0:T(8,128)(2,1)S(1)} %shard_map.37) | data formatting | bytes 1048576

commit v8 on v6

--- a/solution.py
+++ b/solution.py
@@ -220,7 +220,7 @@
     sub = chunk // 2 if chunk >= 2 * HEAD_DIM else chunk
     per_sub = sub // rows
 
-    def attend(at_keys, row0, size, first=False):
+    def attend(at_keys, row0, size, first=False, closing=False):
         keys = kv_all[0, at_keys, :]
         count = keys.shape[0]
         ones = jnp.ones((count, HEAD_DIM), jnp.bfloat16)
@@ -242,12 +242,16 @@
             spread = jnp.concatenate([top] * (count // HEAD_DIM), axis=1)
             weight = jnp.exp2((score - spread) * scale).astype(jnp.bfloat16)
             product = jnp.dot(weight, values, preferred_element_type=jnp.float32)
-            if first:
+            if not first:
+                shrink = jnp.exp2((before - top) * scale)
+                product = summed[at, :] * jnp.concatenate([shrink, shrink], axis=1) + product
+            if closing:
+                result[pl.ds(pl.multiple_of(row0, size), size), j * HEAD_DIM:(j + 1) * HEAD_DIM] = (
+                    product[:, :HEAD_DIM] / product[:, HEAD_DIM:]
+                ).astype(jnp.bfloat16)
+            else:
                 summed[at, :] = product
-            else:
-                shrink = jnp.exp2((before - top) * scale)
-                summed[at, :] = summed[at, :] * jnp.concatenate([shrink, shrink], axis=1) + product
-            largest[at, :] = top
+                largest[at, :] = top
 
     def own_tile(shift):
         for r in range(chunks):
@@ -349,10 +353,11 @@
             for s in range(0, chunk, size):
                 row0 = nearest(shift) * chunk + s
                 if attending:
-                    attend(final, row0, size)
+                    attend(final, row0, size, closing=True)
                 for i in range(size // rows):
                     to = row0 // rows + (me + 1 + i) % (size // rows)
-                    finish(to)
+                    if not attending:
+                        finish(to)
                     if shift:
                         out_copy(me, to, to).start()
                         continue

time: 28 us -> 28 us (level)
  no operation moved by 1% of the time
where the time goes in v8:
time: 28 us; the launch traced here: 27.8 us
  Pallas kernels  27 us (96%)
  local copies, waits for them, and re-layouts  0.8 us (3%)
    pallas_call x1, Pallas kernels, on_device(): pl.pallas_call(functools.partial(kernel, cfg), out_shape=pltpu.VMEM(queri...  27 us
    unnamed x1, local copies, waits for them, and re-layouts  0.8 us

profile of v8, /device:TPU:25, one launch (start us, length us, event | category | flops | bytes accessed | tf_op | source)
XLA Modules:
  0.0 27.8 jit_solution(16109195870058462185)
XLA Ops:
  0.0 27.0 %shard_map.37 = bf16[64,4096]{1,0:T(8,128)(2,1)S(1)} custom-call(bf16[64,4096]{1,0:T(8,128)(2,1)} %q_in.1, bf16[64,1024]{1,0:T(8,128)(2,1)} %k_in.1, bf16[64,1024]{1,0:T(8,128)(2,1)} %v_in.1), custom_call_target="tpu_custom_call" | custom-call | tf_op jit(solution)/shard_map/pallas_call | solution.py:419
  27.0 0.8 %copy.5 = bf16[64,4096]{1,0:T(8,128)(2,1)} copy(bf16[64,4096]{1,0:T(8,128)(2,1)S(1)} %shard_map.37) | data formatting | bytes 1048576

commit v9 on v6

--- a/solution.py
+++ b/solution.py
@@ -168,13 +168,13 @@
     wait_all(q_stage, load_sem.at[1])
 
     for side in range(1 + max(core_of.values())):
-        start_all(kv_copy, [m for m in far_first if core_of[m] == side])
-
         @pl.when(has_up)
         def _(side=side):
             for mask in far_first:
                 if core_of[mask] == side:
                     rise_copy(peer(mask)).start()
+
+        start_all(kv_copy, [m for m in far_first if core_of[m] == side])
 
         start_all(q_copy, [m for m in near_first if core_of[m] == side])
 

time: 28 us -> 28 us (level)
  no operation moved by 1% of the time
where the time goes in v9:
time: 28 us; the launch traced here: 27.8 us
  Pallas kernels  27 us (96%)
  local copies, waits for them, and re-layouts  0.8 us (3%)
    pallas_call x1, Pallas kernels, on_device(): pl.pallas_call(functools.partial(kernel, cfg), out_shape=pltpu.VMEM(queri...  27 us
    unnamed x1, local copies, waits for them, and re-layouts  0.8 us

profile of v9, /device:TPU:25, one launch (start us, length us, event | category | flops | bytes accessed | tf_op | source)
XLA Modules:
  0.0 27.8 jit_solution(18356376700000567592)
XLA Ops:
  0.0 27.0 %shard_map.37 = bf16[64,4096]{1,0:T(8,128)(2,1)S(1)} custom-call(bf16[64,4096]{1,0:T(8,128)(2,1)} %q_in.1, bf16[64,1024]{1,0:T(8,128)(2,1)} %k_in.1, bf16[64,1024]{1,0:T(8,128)(2,1)} %v_in.1), custom_call_target="tpu_custom_call" | custom-call | tf_op jit(solution)/shard_map/pallas_call | solution.py:414
  27.0 0.8 %copy.5 = bf16[64,4096]{1,0:T(8,128)(2,1)} copy(bf16[64,4096]{1,0:T(8,128)(2,1)S(1)} %shard_map.37) | data formatting | bytes 1048576
